TPU v7x, 32 devices: a whole 2x2x4 slice. The times are simulated.
32 devices in a mesh: ctx: 8 (over y, x, core), wsh: 4 (over z).
Axes of the slice: x: 2, y: 2, z: 4, core: 2. Of those that a mesh axis runs over, the one named last changes fastest.
Arguments:
- tokens: bfloat16 [4, 1024, 1792], P('wsh', 'ctx'), may hold values from -6 to 6
- cotangent: bfloat16 [4, 1024, 1792], P('wsh', 'ctx'), may hold values from -6 to 6
- segment_ids: int32 [4, 1024], P('wsh'), may hold values from 0 to 23, never falling along the last dimension, each value on 1 to 256 neighbouring positions
- block_order: int32 [16], replicated, may hold values from 0 to 15, as said below
- premix: float32 [1792], P(('ctx', 'wsh')), may hold values from 0.5 to 1.5
- inward: float32 [1792, 2304], P(('ctx', 'wsh')), may hold values from -0.125 to 0.125
- filters: float32 [3, 1792], P(None, ('ctx', 'wsh')), may hold values from -4 to 4
- outward: float32 [1792, 1792], P(('ctx', 'wsh')), may hold values from -1 to 1
- prefeed: float32 [1792], P(('ctx', 'wsh')), may hold values from 0.5 to 1.5
- expand: float32 [1792, 9728], P(('ctx', 'wsh')), may hold values from -0.125 to 0.125
- shrink: float32 [4864, 1792], P(('ctx', 'wsh')), may hold values from -0.078125 to 0.078125
- premix_state: float32 [2, 1792], P(None, ('ctx', 'wsh')), may hold values from -30 to 100, as said below
- inward_state: float32 [2, 1792, 2304], P(None, ('ctx', 'wsh')), may hold values from -30 to 100, as said below
- filters_state: float32 [2, 3, 1792], P(None, None, ('ctx', 'wsh')), may hold values from -30 to 100, as said below
- outward_state: float32 [2, 1792, 1792], P(None, ('ctx', 'wsh')), may hold values from -30 to 100, as said below
- prefeed_state: float32 [2, 1792], P(None, ('ctx', 'wsh')), may hold values from -30 to 100, as said below
- expand_state: float32 [2, 1792, 9728], P(None, ('ctx', 'wsh')), may hold values from -30 to 100, as said below
- shrink_state: float32 [2, 4864, 1792], P(None, ('ctx', 'wsh')), may hold values from -30 to 100, as said below
Outputs:
- block_output: bfloat16 [4, 1024, 1792], P('wsh', 'ctx')
- input_grad: bfloat16 [4, 1024, 1792], P('wsh', 'ctx')
- premix_grad: float32 [1792], P(('ctx', 'wsh'))
- inward_grad: float32 [1792, 2304], P(('ctx', 'wsh'))
- filters_grad: float32 [3, 1792], P(None, ('ctx', 'wsh'))
- outward_grad: float32 [1792, 1792], P(('ctx', 'wsh'))
- prefeed_grad: float32 [1792], P(('ctx', 'wsh'))
- expand_grad: float32 [1792, 9728], P(('ctx', 'wsh'))
- shrink_grad: float32 [4864, 1792], P(('ctx', 'wsh'))
- premix_moments: float32 [2, 1792], P(None, ('ctx', 'wsh'))
- inward_moments: float32 [2, 1792, 2304], P(None, ('ctx', 'wsh'))
- filters_moments: float32 [2, 3, 1792], P(None, None, ('ctx', 'wsh'))
- outward_moments: float32 [2, 1792, 1792], P(None, ('ctx', 'wsh'))
- prefeed_moments: float32 [2, 1792], P(None, ('ctx', 'wsh'))
- expand_moments: float32 [2, 1792, 9728], P(None, ('ctx', 'wsh'))
- shrink_moments: float32 [2, 4864, 1792], P(None, ('ctx', 'wsh'))
- premix_master: float32 [1792], P(('ctx', 'wsh'))
- inward_master: float32 [1792, 2304], P(('ctx', 'wsh'))
- filters_master: float32 [3, 1792], P(None, ('ctx', 'wsh'))
- outward_master: float32 [1792, 1792], P(('ctx', 'wsh'))
- prefeed_master: float32 [1792], P(('ctx', 'wsh'))
- expand_master: float32 [1792, 9728], P(('ctx', 'wsh'))
- shrink_master: float32 [4864, 1792], P(('ctx', 'wsh'))
- weight_norms: float32 [2, 7], replicated
Inputs may be any that keep to these rules, and one draw needn't show every extreme that they name: `segment_ids`: each sequence's segment numbers never fall along positions and start at 0; a segment holds at most 256 positions and one holds exactly that many. `block_order`: A permutation of the 16 blocks; the two slots of each index of ctx hold blocks b and 15 - b for some b. `premix_state`: index 0 holds first moments, index 1 second moments, which are positive. `inward_state`: index 0 holds first moments, index 1 second moments, which are positive. `filters_state`: index 0 holds first moments, index 1 second moments, which are positive. `outward_state`: index 0 holds first moments, index 1 second moments, which are positive. `prefeed_state`: index 0 holds first moments, index 1 second moments, which are positive. `expand_state`: index 0 holds first moments, index 1 second moments, which are positive. `shrink_state`: index 0 holds first moments, index 1 second moments, which are positive.
All inputs are finite; a program needn't handle non-finite values.
Results may differ from a plain program's by a relative error of at most 0.013.
The roundings to bfloat16 on the way count: a program that leaves them out, or rounds other values in their place, can miss the bound.
Values may be sent and summed in bfloat16 or wider, within the bound.
A program may use at most 320 MiB of HBM per device.

v0:
```python
import jax
import jax.numpy as jnp
from jax import lax
from jax.sharding import PartitionSpec as P

HEADS = 16
QUERY_KEY_WIDTH = 16
KCONV = 3
STEP = 3
HDV = 112
QK = 256
TILE = 128
norm_eps = 1e-05
adam_eps = 1e-08
beta_first = 0.9
beta_second = 0.99
learn_rate = 0.5
f32 = jnp.float32
bf16 = jnp.bfloat16
BOTH = ("ctx", "wsh")


def mm(left, right):
    return jnp.dot(left, right, preferred_element_type=f32)


def mm_nt(left, right):
    return lax.dot_general(left, right, (((1,), (1,)), ((), ())), preferred_element_type=f32)


def mm_tn(left, right):
    return lax.dot_general(left, right, (((0,), (0,)), ((), ())), preferred_element_type=f32)


def inverse_rms(values):
    return lax.rsqrt(jnp.mean(values * values, axis=-1, keepdims=True) + norm_eps)


def rms_back(grad_normed, normed, scaler):
    return scaler * (grad_normed - normed * jnp.mean(grad_normed * normed, axis=-1, keepdims=True))


def silu_slope(values):
    sigmoid = jax.nn.sigmoid(values)
    return sigmoid * (1.0 + values * (1.0 - sigmoid))


def gather_rows(values):
    return lax.all_gather(values, "ctx", axis=0, tiled=True)


def scatter_sum(values, ctx):
    rows, columns = values.shape
    pieces = lax.all_to_all(values.reshape(ctx, rows // ctx, columns), "ctx", 0, 0)
    return jnp.sum(pieces.astype(f32), axis=0)


def split_columns(shard, parts, ctx):
    rows = shard.shape[0]
    pieces, start = ([], 0)
    for width in parts:
        piece = shard[:, start : start + width].reshape(rows, ctx, width // ctx)
        pieces.append(piece)
        start += width
    return jnp.transpose(jnp.concatenate(pieces, axis=2), (1, 0, 2))


def join_columns(pieces, parts, ctx):
    moved = jnp.transpose(pieces, (1, 0, 2))
    rows, joined, start = (moved.shape[0], [], 0)
    for width in parts:
        own = width // ctx
        joined.append(moved[:, :, start : start + own].reshape(rows, width))
        start += own
    return jnp.concatenate(joined, axis=1)


def gather_columns(shard, parts, ctx):
    pieces = split_columns(shard, parts, ctx)
    rows, columns = pieces.shape[1:]
    swapped = lax.all_to_all(pieces, "ctx", 0, 0)
    full = lax.all_gather(swapped, "wsh", axis=1)
    return full.reshape(-1, columns)


def return_columns(grad, parts, ctx, wsh):
    columns = grad.shape[1]
    pieces = grad.astype(bf16).reshape(ctx, wsh, -1, columns)
    swapped = lax.all_to_all(pieces, "wsh", 1, 0)
    summed = jnp.sum(swapped.astype(f32), axis=0).astype(bf16)
    back = lax.all_to_all(summed, "ctx", 0, 0)
    return join_columns(back, parts, ctx).astype(f32)


def return_rows(grad, wsh):
    columns = grad.shape[1]
    pieces = grad.astype(bf16).reshape(wsh, -1, columns)
    swapped = lax.all_to_all(pieces, "wsh", 0, 0)
    return jnp.sum(swapped.astype(f32), axis=0)


def windows(values, prior):
    tiles = values.reshape((-1, TILE) + values.shape[1:])
    count = tiles.shape[0]
    padded = jnp.concatenate([jnp.zeros((prior,) + tiles.shape[1:], values.dtype), tiles], axis=0)
    return jnp.concatenate([padded[j : j + count] for j in range(prior + 1)], axis=1)


def unwindow(grads, prior):
    count = grads.shape[0]
    tail = grads.shape[2:]
    pieces = grads.reshape((count, prior + 1, TILE) + tail)
    total = jnp.zeros((count + prior, TILE) + tail, grads.dtype)
    for j in range(prior + 1):
        total = total.at[j : j + count].add(pieces[:, j])
    return total[prior:].reshape((count * TILE,) + tail)


def scores_of(query_tiles, key_windows, allowed):
    scores = jnp.einsum(
        "tqhd,tkhd->htqk", query_tiles, key_windows, preferred_element_type=f32
    ) * QUERY_KEY_WIDTH ** (-0.5)
    return (scores, (1.0 + scores + 0.5 * scores * scores) * allowed[None])


def allowed_of(segments, prior):
    length = segments.shape[0]
    positions = jnp.arange(length, dtype=jnp.int32)
    key_pos = jnp.arange(length, dtype=jnp.int32) + 1
    key_windows = windows(key_pos, prior)
    seg_windows = windows(segments, prior)
    pos_tiles = positions.reshape(-1, TILE)
    seg_tiles = segments.reshape(-1, TILE)
    return (
        (key_windows[:, None, :] >= 1)
        & (key_windows[:, None, :] - 1 <= pos_tiles[:, :, None])
        & (seg_windows[:, None, :] == seg_tiles[:, :, None])
    ).astype(f32)


def shifted(values, offset):
    if offset == 0:
        return values
    rows = values.shape[0]
    edge = jnp.zeros((abs(offset),) + values.shape[1:], values.dtype)
    if offset > 0:
        return jnp.concatenate([edge, values[: rows - offset]], axis=0)
    return jnp.concatenate([values[-offset:], edge], axis=0)


def make_body(ctx, wsh):

    def body(
        tokens,
        cotangent,
        segment_ids,
        block_order,
        premix,
        inward,
        filters,
        outward,
        prefeed,
        expand,
        shrink,
        premix_state,
        inward_state,
        filters_state,
        outward_state,
        prefeed_state,
        expand_state,
        shrink_state,
    ):
        masters = (premix, inward, filters, outward, prefeed, expand, shrink)
        states = (
            premix_state,
            inward_state,
            filters_state,
            outward_state,
            prefeed_state,
            expand_state,
            shrink_state,
        )
        width = tokens.shape[2]
        feed = expand.shape[1] // 2
        segments = segment_ids[0]
        length = segments.shape[0]
        blocks = block_order.shape[0]
        block_rows = length // blocks
        prior = -(-(length // 4 - 1) // TILE)
        heads = HEADS // ctx
        keys_width = QK // ctx
        own_values = width // ctx
        own_feed = feed // ctx
        inverse = (
            jnp.zeros((blocks,), jnp.int32).at[block_order].set(jnp.arange(blocks, dtype=jnp.int32))
        )

        def reorder(values, indices):
            return jnp.take(values.reshape(blocks, block_rows, -1), indices, axis=0).reshape(
                length, -1
            )

        in_parts, ex_parts = ((QK, QK, width), (feed, feed))
        gains = lax.all_gather(
            jnp.stack([premix, prefeed]).astype(bf16), BOTH, axis=1, tiled=True
        ).astype(f32)
        gain_one, gain_two = (gains[0], gains[1])
        taps = lax.all_gather(filters.astype(bf16), "wsh", axis=1, tiled=True).astype(f32)
        inward_own = gather_columns(inward.astype(bf16), in_parts, ctx)
        outward_own = lax.all_gather(outward.astype(bf16), "wsh", axis=0, tiled=True)
        expand_own = gather_columns(expand.astype(bf16), ex_parts, ctx)
        shrink_own = lax.all_gather(shrink.astype(bf16), "wsh", axis=0, tiled=True)
        tokens_all = gather_rows(tokens[0])
        grad_ffn = gather_rows(cotangent[0])
        inputs_all = tokens_all.astype(f32)
        mixed_in = (inputs_all * inverse_rms(inputs_all) * gain_one).astype(bf16)
        project = reorder(mm(mixed_in, inward_own).astype(bf16), inverse)
        queries = project[:, :keys_width].reshape(-1, TILE, heads, QUERY_KEY_WIDTH)
        keys = project[:, keys_width : 2 * keys_width].reshape(length, heads, QUERY_KEY_WIDTH)
        values = project[:, 2 * keys_width :]
        value_float = values.astype(f32)
        usable, tapped = ([], [])
        for offset in range(KCONV):
            usable.append(
                ((shifted(segments, offset) == segments) & (jnp.arange(length) >= offset)).astype(
                    f32
                )[:, None]
            )
            tapped.append(shifted(value_float, offset) * usable[offset])
        convolved = sum((taps[offset] * tapped[offset] for offset in range(KCONV)))
        allowed = allowed_of(segments, prior)
        key_windows = windows(keys, prior)
        value_windows = windows(values.reshape(length, heads, HDV), prior)
        scores, weights = scores_of(queries, key_windows, allowed)
        probs = weights.astype(bf16)
        totals = jnp.sum(weights, axis=3)
        totals_rows = jnp.transpose(totals, (1, 2, 0))[..., None]
        numer = jnp.einsum("htqk,tkhd->tqhd", probs, value_windows, preferred_element_type=f32)
        attended = numer / totals_rows
        attended_flat = attended.reshape(length, own_values)
        conv_gate = jax.nn.silu(convolved)
        gated = reorder((attended_flat * conv_gate).astype(bf16), block_order)
        mixed_out = mm(gated, outward_own).astype(bf16)
        inputs = tokens[0].astype(f32)
        residual = inputs + scatter_sum(mixed_out, ctx)
        scaler_two = inverse_rms(residual)
        normed_two = residual * scaler_two
        feed_in = gather_rows((normed_two * gain_two).astype(bf16))
        gate_up = mm(feed_in, expand_own)
        gate_part, up_part = (gate_up[:, :own_feed], gate_up[:, own_feed:])
        gate_silu = jax.nn.silu(gate_part)
        activated = (gate_silu * up_part).astype(bf16)
        block_output = (residual + scatter_sum(mm(activated, shrink_own).astype(bf16), ctx)).astype(
            bf16
        )
        shrink_grad = mm_tn(activated, grad_ffn)
        grad_act = mm_nt(grad_ffn, shrink_own)
        grad_gate_up = jnp.concatenate(
            [grad_act * up_part * silu_slope(gate_part), grad_act * gate_silu], axis=1
        ).astype(bf16)
        expand_grad = mm_tn(feed_in, grad_gate_up)
        grad_feed = scatter_sum(mm_nt(grad_gate_up, expand_own).astype(bf16), ctx)
        prefeed_part = jnp.sum(grad_feed * normed_two, axis=0)
        grad_resid = cotangent[0].astype(f32) + rms_back(
            grad_feed * gain_two, normed_two, scaler_two
        )
        grad_mix = gather_rows(grad_resid.astype(bf16))
        outward_grad = mm_tn(gated, grad_mix)
        grad_gated = reorder(mm_nt(grad_mix, outward_own), inverse)
        grad_attended = (grad_gated * conv_gate).reshape(-1, TILE, heads, HDV)
        grad_conv = grad_gated * attended_flat * silu_slope(convolved)
        filters_part = jnp.stack(
            [jnp.sum(grad_conv * tapped[offset], axis=0) for offset in range(KCONV)]
        )
        grad_numer = (grad_attended / totals_rows).astype(bf16)
        grad_totals = -jnp.sum(grad_attended * attended, axis=3) / totals_rows[..., 0]
        grad_totals = jnp.transpose(grad_totals, (2, 0, 1))
        grad_weights = (
            jnp.einsum("tqhd,tkhd->htqk", grad_numer, value_windows, preferred_element_type=f32)
            + grad_totals[..., None]
        )
        score_gradient = (grad_weights * (1.0 + scores) * allowed[None]).astype(bf16)
        scale = QUERY_KEY_WIDTH ** (-0.5)
        grad_query = (
            jnp.einsum("htqk,tkhd->tqhd", score_gradient, key_windows, preferred_element_type=f32)
            * scale
        )
        grad_keys = (
            unwindow(
                jnp.einsum("htqk,tqhd->tkhd", score_gradient, queries, preferred_element_type=f32),
                prior,
            )
            * scale
        )
        grad_values = unwindow(
            jnp.einsum("htqk,tqhd->tkhd", probs, grad_numer, preferred_element_type=f32), prior
        ).reshape(length, own_values)
        for offset in range(KCONV):
            grad_values = grad_values + taps[offset] * shifted(grad_conv * usable[offset], -offset)
        grad_project = reorder(
            jnp.concatenate(
                [
                    grad_query.reshape(length, keys_width),
                    grad_keys.reshape(length, keys_width),
                    grad_values,
                ],
                axis=1,
            ).astype(bf16),
            block_order,
        )
        inward_grad = mm_tn(mixed_in, grad_project)
        grad_mixin = scatter_sum(mm_nt(grad_project, inward_own).astype(bf16), ctx)
        scaler_one = inverse_rms(inputs)
        normed_one = inputs * scaler_one
        premix_part = jnp.sum(grad_mixin * normed_one, axis=0)
        input_grad = (grad_resid + rms_back(grad_mixin * gain_one, normed_one, scaler_one)).astype(
            bf16
        )
        gain_grads = lax.psum_scatter(
            jnp.stack([premix_part, prefeed_part]), BOTH, scatter_dimension=1, tiled=True
        )
        shards = (
            gain_grads[0],
            return_columns(inward_grad, in_parts, ctx, wsh),
            lax.psum_scatter(filters_part, "wsh", scatter_dimension=1, tiled=True),
            return_rows(outward_grad, wsh),
            gain_grads[1],
            return_columns(expand_grad, ex_parts, ctx, wsh),
            return_rows(shrink_grad, wsh),
        )
        return (block_output[None], input_grad[None]) + shards + update(masters, states, shards)

    return body


def update(masters, states, shards):
    moments = []
    directions = []
    for state_pair, gradient in zip(states, shards):
        first_moment = beta_first * state_pair[0] + (1.0 - beta_first) * gradient
        second = beta_second * state_pair[1] + (1.0 - beta_second) * gradient * gradient
        directions.append(
            first_moment
            / (1.0 - beta_first**STEP)
            / (jnp.sqrt(second / (1.0 - beta_second**STEP)) + adam_eps)
        )
        moments.append(jnp.stack([first_moment, second]))
    step_sums = jnp.stack([jnp.sum(direction * direction) for direction in directions])
    weight_sums = jnp.stack([jnp.sum(weight * weight) for weight in masters])
    totals = lax.psum(jnp.stack([weight_sums, step_sums]), BOTH)
    norms = jnp.sqrt(totals)
    updated = [
        masters[i] - learn_rate * (norms[0, i] / norms[1, i]) * directions[i] for i in range(7)
    ]
    return tuple(moments) + tuple(updated) + (norms,)


def solution(mesh):
    ctx, wsh = (mesh.shape["ctx"], mesh.shape["wsh"])
    rows, columns, moments_rows = (P(BOTH, None), P(None, BOTH), P(None, BOTH, None))
    vector, whole = (P(BOTH), P("wsh", "ctx", None))
    weights = (vector, rows, columns, rows, vector, rows, rows)
    states = (
        columns,
        moments_rows,
        P(None, None, BOTH),
        moments_rows,
        columns,
        moments_rows,
        moments_rows,
    )
    return jax.shard_map(
        make_body(ctx, wsh),
        mesh=mesh,
        in_specs=(whole, whole, P("wsh", None), P()) + weights + states,
        out_specs=(whole, whole) + weights + states + weights + (P(),),
        check_vma=False,
    )
```

profile of v0, /device:TPU:0, one launch (start us, length us, event | category | flops | bytes accessed | tf_op | source)
XLA Modules:
  0.0 969.0 jit_solution(15023815569160416463)
XLA Ops:
  10.8 5.2 all-to-all-start
  16.7 69.3 %all-gather.4 = bf16[32,56,2]{1,2,0:T(2,128)(2,1)S(1)} all-gather(bf16[1,56,2]{1,2,0:T(2,128)(2,1)S(1)} %maximum_bitcast_fusion.2), channel_id=1, replica_groups=mesh['ctx'=8,'wsh'=4] {'ctx','wsh'}, dimensions={0}, use_global_device_ids=true | all-gather | bytes 7392 | tf_op jit(solution)/shard_map/all_gather | solution.py:204
  86.7 7.6 all-gather.5
  103.6 4.2 all-to-all-start.2
  109.2 18.9 %all_gather.41 = bf16[224,1792]{1,0:T(8,128)(2,1)} all-gather(bf16[56,1792]{1,0:T(8,128)(2,1)S(1)} %get-tuple-element.311), channel_id=1, replica_groups=mesh['ctx'=8,'wsh'=4] {'wsh'}, dimensions={0}, use_global_device_ids=true | all-gather | bytes 1003520 | tf_op jit(solution)/shard_map/all_gather | solution.py:210
  129.0 24.9 %all-gather.1 = bf16[8,224,288]{2,0,1:T(8,128)(2,1)S(1)} all-gather(bf16[8,56,288]{2,0,1:T(8,128)(2,1)S(1)} %copy.320), channel_id=3, replica_groups=mesh['ctx'=8,'wsh'=4] {'wsh'}, dimensions={1}, use_global_device_ids=true | all-gather | bytes 1290240 | tf_op jit(solution)/shard_map/all_gather | solution.py:82
  184.7 47.2 %all_to_all.68 = bf16[8,128,1792]{2,1,0:T(8,128)(2,1)S(1)} all-to-all(bf16[8,128,1792]{2,1,0:T(8,128)(2,1)S(1)} %bitcast.354), channel_id=1, replica_groups=mesh['ctx'=8,'wsh'=4] {'ctx'}, dimensions={0} | all-to-all | bytes 7340032 | tf_op jit(solution)/shard_map/all_to_all | solution.py:54
  237.0 9.8 %all-gather.21.cloned.1.call-done = bf16[8,224,1216]{2,1,0:T(8,128)(2,1)} async-done(((bf16[8,56,1216]{2,1,0:T(8,128)(2,1)}), bf16[8,224,1216]{2,1,0:T(8,128)(2,1)}) %all-gather.21.cloned.1.call-update) | async-done | bytes 4358160 | tf_op jit(solution)/shard_map/all_gather | solution.py:82
  246.8 35.3 %all-gather.13.cloned.1.call-done = bf16[1024,1792]{1,0:T(8,128)(2,1)} async-done(((bf16[128,1792]{1,0:T(8,128)(2,1)}), bf16[1024,1792]{1,0:T(8,128)(2,1)}) %all-gather.13.cloned.1.call-update) | async-done | bytes 3670032 | tf_op jit(solution)/shard_map/all_gather | solution.py:49
  282.1 10.4 %fusion.142 = f32[1024,1216]{0,1:T(8,128)} fusion(bf16[1024,1792]{1,0:T(8,128)(2,1)} %all-gather.13.cloned.1.call-done, bf16[1792,1216]{1,0:T(8,128)(2,1)} %bitcast.412), kind=kOutput, calls=%fused_computation.307 | convolution fusion | flops 4462739456 | bytes 13008896 | tf_op jit(solution)/shard_map/dot_general | solution.py:24
  292.5 38.6 %all-gather.15.cloned.1.call-done = bf16[608,1792]{1,0:T(8,128)(2,1)} async-done(((bf16[152,1792]{1,0:T(8,128)(2,1)}), bf16[608,1792]{1,0:T(8,128)(2,1)}) %all-gather.15.cloned.1.call-update) | async-done | bytes 2179088 | tf_op jit(solution)/shard_map/all_gather | solution.py:212
  331.1 34.9 %all-gather.23.cloned.1.call-done = bf16[1,1024,1792]{2,1,0:T(8,128)(2,1)} async-done(((bf16[1,128,1792]{2,1,0:T(8,128)(2,1)}), bf16[1,1024,1792]{2,1,0:T(8,128)(2,1)}) %all-gather.23.cloned.1.call-update) | async-done | bytes 3670032 | tf_op jit(solution)/shard_map/all_gather | solution.py:49
  366.1 8.4 multiply_convert_fusion.2
  374.4 9.7 convolution_convert_fusion.2
  384.1 4.7 all-to-all-start.4
  388.8 6.9 convolution_convert_fusion.3
  395.8 36.6 %all-to-all-done.4 = bf16[8,128,1792]{2,1,0:T(8,128)(2,1)} async-done(((bf16[8,128,1792]{2,1,0:T(8,128)(2,1)}), bf16[8,128,1792]{2,1,0:T(8,128)(2,1)}, u32[]{:S(2)}, u32[]{:S(2)}) %all-to-all-start.4) | async-done | bytes 3670048 | tf_op jit(solution)/shard_map/all_to_all | solution.py:54
  432.3 4.5 all-to-all-start.3
  436.8 6.2 fusion.7
  443.0 37.3 %all-to-all-done.3 = bf16[8,128,1792]{2,1,0:T(8,128)(2,1)} async-done(((bf16[8,128,1792]{2,1,0:T(8,128)(2,1)}), bf16[8,128,1792]{2,1,0:T(8,128)(2,1)}, u32[]{:S(2)}, u32[]{:S(2)}) %all-to-all-start.3) | async-done | bytes 3670048 | tf_op jit(solution)/shard_map/all_to_all | solution.py:54
  480.3 4.6 all-to-all-start.11
  484.9 9.6 convolution_convert_fusion
  494.5 7.2 copy.370
  501.6 4.7 copy.371
  506.4 25.8 %all-to-all-done.11 = bf16[4,152,1792]{2,1,0:T(8,128)(2,1)} async-done(((bf16[4,152,1792]{2,1,0:T(8,128)(2,1)}), bf16[4,152,1792]{2,1,0:T(8,128)(2,1)}, u32[]{:S(2)}, u32[]{:S(2)}) %all-to-all-start.11) | async-done | bytes 2179104 | tf_op jit(solution)/shard_map/all_to_all | solution.py:98
  532.1 4.9 all-to-all-start.9
  545.4 5.0 stack.155
  557.9 80.3 %all-to-all-done.9 = bf16[1,8,4,56,1216]{4,3,1,0,2:T(8,128)(2,1)} async-done(((bf16[1,8,4,56,1216]{4,3,1,0,2:T(8,128)(2,1)}), bf16[1,8,4,56,1216]{4,3,1,0,2:T(8,128)(2,1)}, u32[]{:S(2)}, u32[]{:S(2)}) %all-to-all-start.9) | async-done | bytes 4358176 | tf_op jit(solution)/shard_map/all_to_all | solution.py:89
  638.2 4.4 reduce_sum.346
  642.6 4.9 all-to-all-start.10
  654.2 9.9 %all-to-all-done.10 = bf16[8,56,1216]{2,1,0:T(8,128)(2,1)} async-done(((bf16[8,56,1216]{2,1,0:T(8,128)(2,1)}), bf16[8,56,1216]{2,1,0:T(8,128)(2,1)}, u32[]{:S(2)}, u32[]{:S(2)}) %all-to-all-start.10) | async-done | bytes 1089568 | tf_op jit(solution)/shard_map/all_to_all | solution.py:91
  670.3 4.4 fusion.143
  677.6 4.4 multiply_reduce_fusion.6
  722.0 4.5 convolution_convert_fusion.5
  729.5 4.3 all-to-all-start.6
  733.8 4.5 fusion.11
  743.1 6.9 multiply_reduce_fusion
  751.9 12.1 %all-to-all-done.6 = bf16[1,8,4,56,288]{4,3,1,0,2:T(8,128)(2,1)} async-done(((bf16[1,8,4,56,288]{4,3,1,0,2:T(8,128)(2,1)}), bf16[1,8,4,56,288]{4,3,1,0,2:T(8,128)(2,1)}, u32[]{:S(2)}, u32[]{:S(2)}) %all-to-all-start.6) | async-done | bytes 1032224 | tf_op jit(solution)/shard_map/all_to_all | solution.py:89
  764.0 4.2 all-to-all-start.8
  768.3 4.0 pad_maximum_fusion
  772.3 15.3 %all-reduce.12 = f32[3,224]{1,0:T(4,128)} all-reduce(f32[3,224]{1,0:T(4,128)S(1)} %pad_maximum_fusion.13), channel_id=7, replica_groups=mesh['ctx'=8,'wsh'=4] {'wsh'}, use_global_device_ids=true, to_apply=%region_19.21.clone | all-reduce | flops 672 | bytes 5376
  790.0 5.2 all-to-all-start.7
  795.2 3.9 convolution_convert_fusion.1
  803.0 4.6 all-to-all-start.5
  818.2 32.9 %all-to-all-done.5 = bf16[8,128,1792]{2,1,0:T(8,128)(2,1)} async-done(((bf16[8,128,1792]{2,1,0:T(8,128)(2,1)}), bf16[8,128,1792]{2,1,0:T(8,128)(2,1)}, u32[]{:S(2)}, u32[]{:S(2)}) %all-to-all-start.5) | async-done | bytes 3670048 | tf_op jit(solution)/shard_map/all_to_all | solution.py:54
  854.1 42.1 %all-reduce.11 = f32[2,1792]{1,0:T(2,128)S(1)} all-reduce(f32[2,1792]{1,0:T(2,128)S(1)} %pad_maximum_fusion.12), channel_id=6, replica_groups=mesh['ctx'=8,'wsh'=4] {'ctx','wsh'}, use_global_device_ids=true, to_apply=%region_14.16.clone | all-reduce | flops 3584 | bytes 28672
  897.5 4.6 stack.164
  902.1 39.1 %psum.7 = f32[2,7]{1,0:T(2,128)S(1)} all-reduce(f32[2,7]{1,0:T(2,128)S(1)} %pad_maximum_fusion.17), channel_id=1, replica_groups=mesh['ctx'=8,'wsh'=4] {'ctx','wsh'}, use_global_device_ids=true, to_apply=%region_37.39 | all-reduce | flops 14 | bytes 112 | tf_op jit(solution)/shard_map/psum | solution.py:350
  (405 shorter events, 164.5 us)
Async XLA Ops:
  7.2 152.1 %all-gather.19.cloned.1.call-start = ((), (), s32[]{:S(2)}) async-start(), calls=%async_computation.15 | async-start | bytes 4128768 | tf_op jit(solution)/shard_map/all_gather | solution.py:49
  7.9 8.1 copy-start.93
  7.9 8.1 copy-start.95
  9.3 76.8 %copy-start.70 = (f32[3,56]{1,0:T(4,128)S(1)}, f32[3,56]{1,0:T(4,128)}, u32[]{:S(2)}) copy-start(f32[3,56]{1,0:T(4,128)} %param.38) | copy-start | bytes 2020
  9.3 85.0 %copy-start.8 = (f32[56,9728]{1,0:T(8,128)S(1)}, f32[56,9728]{1,0:T(8,128)}, u32[]{:S(2)}) copy-start(f32[56,9728]{1,0:T(8,128)} %param.41) | copy-start | bytes 6537220
  10.8 92.8 %all-to-all-start = ((bf16[8,56,288]{2,1,0:T(8,128)(2,1)}), bf16[8,56,288]{2,1,0:T(8,128)(2,1)}, u32[]{:S(2)}, u32[]{:S(2)}) async-start(bf16[8,56,288]{2,1,0:T(8,128)(2,1)} %maximum_bitcast_fusion.1), calls=%async_computation | async-start | bytes 688128 | tf_op jit(solution)/shard_map/all_to_all | solution.py:81
  99.8 440.7 %copy-start.52 = (f32[1792]{0:T(1024)}, f32[1792]{0:T(1024)S(1)}, u32[]{:S(2)}) copy-start(f32[1792]{0:T(1024)S(1)} %get-tuple-element.250) | copy-start | bytes 21508
  99.8 621.4 %copy-start.55 = (f32[1792]{0:T(1024)}, f32[1792]{0:T(1024)S(1)}, u32[]{:S(2)}) copy-start(f32[1792]{0:T(1024)S(1)} %get-tuple-element.249) | copy-start | bytes 21508
  100.3 7.6 copy-start.76
  103.6 55.3 %all-to-all-start.2 = ((bf16[8,56,1216]{2,1,0:T(8,128)(2,1)}), bf16[8,56,1216]{2,1,0:T(8,128)(2,1)}, u32[]{:S(2)}, u32[]{:S(2)}) async-start(bf16[8,56,1216]{2,1,0:T(8,128)(2,1)} %maximum_bitcast_fusion), calls=%async_computation.2 | async-start | bytes 2293760 | tf_op jit(solution)/shard_map/all_to_all | solution.py:81
  107.9 138.9 %all-gather.21.cloned.1.call-start = ((), (), s32[]{:S(2)}) async-start(), calls=%async_computation.16 | async-start | bytes 5734400 | tf_op jit(solution)/shard_map/all_gather | solution.py:82
  109.2 58.7 %copy-start.11 = (f32[8,128,384]{2,1,0:T(8,128)}, f32[8,128,384]{2,1,0:T(8,128)S(1)}, u32[]{:S(2)}) copy-start(f32[8,128,384]{2,1,0:T(8,128)S(1)} %and_convert_fusion) | copy-start | bytes 4718596
  159.0 123.1 %all-gather.13.cloned.1.call-start = ((), (), s32[]{:S(2)}) async-start(), calls=%async_computation.12 | async-start | bytes 4128768 | tf_op jit(solution)/shard_map/all_gather | solution.py:49
  167.3 12.2 %copy-start.4 = (bf16[16,64,288]{2,1,0:T(8,128)(2,1)}, bf16[16,64,288]{2,1,0:T(8,128)(2,1)S(1)}, u32[]{:S(2)}) copy-start(bf16[16,64,288]{2,1,0:T(8,128)(2,1)S(1)} %broadcast_select_fusion.1) | copy-start | bytes 1769476
  234.7 96.4 %all-gather.15.cloned.1.call-start = ((), (), s32[]{:S(2)}) async-start(), calls=%async_computation.13 | async-start | bytes 2723840 | tf_op jit(solution)/shard_map/all_gather | solution.py:212
  236.4 129.7 %all-gather.23.cloned.1.call-start = ((), (), s32[]{:S(2)}) async-start(), calls=%async_computation.17 | async-start | bytes 4128768 | tf_op jit(solution)/shard_map/all_gather | solution.py:49
  374.4 9.7 copy-start.101
  374.4 9.7 copy-start.102
  384.1 48.2 %all-to-all-start.4 = ((bf16[8,128,1792]{2,1,0:T(8,128)(2,1)}), bf16[8,128,1792]{2,1,0:T(8,128)(2,1)}, u32[]{:S(2)}, u32[]{:S(2)}) async-start(bf16[8,128,1792]{2,1,0:T(8,128)(2,1)} %bitcast.366), calls=%async_computation.4 | async-start | bytes 7340032 | tf_op jit(solution)/shard_map/all_to_all | solution.py:54
  432.3 48.0 %all-to-all-start.3 = ((bf16[8,128,1792]{2,1,0:T(8,128)(2,1)}), bf16[8,128,1792]{2,1,0:T(8,128)(2,1)}, u32[]{:S(2)}, u32[]{:S(2)}) async-start(bf16[8,128,1792]{2,1,0:T(8,128)(2,1)} %bitcast.365), calls=%async_computation.3 | async-start | bytes 7340032 | tf_op jit(solution)/shard_map/all_to_all | solution.py:54
  480.3 51.8 %all-to-all-start.11 = ((bf16[4,152,1792]{2,1,0:T(8,128)(2,1)}), bf16[4,152,1792]{2,1,0:T(8,128)(2,1)}, u32[]{:S(2)}, u32[]{:S(2)}) async-start(bf16[4,152,1792]{2,1,0:T(8,128)(2,1)} %bitcast.368), calls=%async_computation.11 | async-start | bytes 4358144 | tf_op jit(solution)/shard_map/all_to_all | solution.py:98
  532.1 106.1 %all-to-all-start.9 = ((bf16[1,8,4,56,1216]{4,3,1,0,2:T(8,128)(2,1)}), bf16[1,8,4,56,1216]{4,3,1,0,2:T(8,128)(2,1)}, u32[]{:S(2)}, u32[]{:S(2)}) async-start(bf16[1,8,4,56,1216]{4,3,1,0,2:T(8,128)(2,1)} %copy.371), calls=%async_computation.9 | async-start | bytes 9175040 | tf_op jit(solution)/shard_map/all_to_all | solution.py:89
  537.1 133.2 %all-gather.17.cloned.1.call-start = ((), (), s32[]{:S(2)}) async-start(), calls=%async_computation.14 | async-start | bytes 4128768 | tf_op jit(solution)/shard_map/all_gather | solution.py:49
  540.4 10.0 %copy-start.89 = (f32[2,3,56]{2,0,1:T(2,128)S(1)}, f32[2,3,56]{2,0,1:T(2,128)}, u32[]{:S(2)}) copy-start(f32[2,3,56]{2,0,1:T(2,128)} %param.45) | copy-start | bytes 4036
  541.3 10.8 %copy-start.90 = (f32[128]{0:T(128)}, f32[128]{0:T(128)S(1)}, u32[]{:S(2)}) copy-start(f32[128]{0:T(128)S(1)} %broadcast_multiply_fusion.1) | copy-start | bytes 1540
  557.9 93.2 %copy-start.5 = (f32[152,1792]{1,0:T(8,128)}, f32[152,1792]{1,0:T(8,128)S(1)}, u32[]{:S(2)}) copy-start(f32[152,1792]{1,0:T(8,128)S(1)} %convert_reduce_fusion.4) | copy-start | bytes 3268612
  642.6 21.5 %all-to-all-start.10 = ((bf16[8,56,1216]{2,1,0:T(8,128)(2,1)}), bf16[8,56,1216]{2,1,0:T(8,128)(2,1)}, u32[]{:S(2)}, u32[]{:S(2)}) async-start(bf16[8,56,1216]{2,1,0:T(8,128)(2,1)} %reduce_sum.346), calls=%async_computation.10 | async-start | bytes 2293760 | tf_op jit(solution)/shard_map/all_to_all | solution.py:91
  665.7 8.9 copy-start.14
  707.5 10.1 %copy-start.65 = (f32[1,224]{1,0:T(1,128)S(1)}, f32[1,224]{1,0:T(1,128)}, u32[]{:S(2)}) copy-start(f32[1,224]{1,0:T(1,128)} %get-tuple-element.316) | copy-start | bytes 2692
  707.5 10.1 %copy-start.67 = (f32[1,224]{1,0:T(1,128)S(1)}, f32[1,224]{1,0:T(1,128)}, u32[]{:S(2)}) copy-start(f32[1,224]{1,0:T(1,128)} %get-tuple-element.317) | copy-start | bytes 2692
  729.5 34.5 %all-to-all-start.6 = ((bf16[1,8,4,56,288]{4,3,1,0,2:T(8,128)(2,1)}), bf16[1,8,4,56,288]{4,3,1,0,2:T(8,128)(2,1)}, u32[]{:S(2)}, u32[]{:S(2)}) async-start(bf16[1,8,4,56,288]{4,3,1,0,2:T(8,128)(2,1)} %copy.363), calls=%async_computation.6 | async-start | bytes 2752512 | tf_op jit(solution)/shard_map/all_to_all | solution.py:89
  764.0 26.0 %all-to-all-start.8 = ((bf16[4,56,1792]{2,1,0:T(8,128)(2,1)}), bf16[4,56,1792]{2,1,0:T(8,128)(2,1)}, u32[]{:S(2)}, u32[]{:S(2)}) async-start(bf16[4,56,1792]{2,1,0:T(8,128)(2,1)} %bitcast.375), calls=%async_computation.8 | async-start | bytes 1605632 | tf_op jit(solution)/shard_map/all_to_all | solution.py:98
  772.3 22.9 %copy-start.39 = (bf16[1792,288]{0,1:T(8,128)(2,1)S(1)}, bf16[1792,288]{0,1:T(8,128)(2,1)}, u32[]{:S(2)}) copy-start(bf16[1792,288]{0,1:T(8,128)(2,1)} %copy-done.38) | copy-start | bytes 3096580
  772.3 22.9 %copy-start.41 = (bf16[16,64,288]{2,1,0:T(8,128)(2,1)S(1)}, bf16[16,64,288]{2,1,0:T(8,128)(2,1)}, u32[]{:S(2)}) copy-start(bf16[16,64,288]{2,1,0:T(8,128)(2,1)} %copy-done.40) | copy-start | bytes 1769476
  790.0 12.9 %all-to-all-start.7 = ((bf16[8,56,288]{2,1,0:T(8,128)(2,1)}), bf16[8,56,288]{2,1,0:T(8,128)(2,1)S(1)}, u32[]{:S(2)}, u32[]{:S(2)}) async-start(bf16[8,56,288]{2,1,0:T(8,128)(2,1)} %reduce_sum.341), calls=%async_computation.7 | async-start | bytes 688128 | tf_op jit(solution)/shard_map/all_to_all | solution.py:91
  803.0 7.8 copy-start.28
  803.0 48.1 %all-to-all-start.5 = ((bf16[8,128,1792]{2,1,0:T(8,128)(2,1)}), bf16[8,128,1792]{2,1,0:T(8,128)(2,1)}, u32[]{:S(2)}, u32[]{:S(2)}) async-start(bf16[8,128,1792]{2,1,0:T(8,128)(2,1)} %bitcast.364), calls=%async_computation.5 | async-start | bytes 7340032 | tf_op jit(solution)/shard_map/all_to_all | solution.py:54
  818.1 35.6 %copy-start.56 = (f32[1792]{0:T(1024)S(1)}, f32[1792]{0:T(1024)}, u32[]{:S(2)}) copy-start(f32[1792]{0:T(1024)} %copy-done.55) | copy-start | bytes 21508
  818.1 35.6 %copy-start.92 = (f32[128]{0:T(128)S(1)}, f32[128]{0:T(128)}, u32[]{:S(2)}) copy-start(f32[128]{0:T(128)} %add_rsqrt_fusion.1) | copy-start | bytes 1540
  818.1 35.9 %copy-start.60 = (f32[1,1792]{1,0:T(1,128)S(1)}, f32[1,1792]{1,0:T(1,128)}, u32[]{:S(2)}) copy-start(f32[1,1792]{1,0:T(1,128)} %stack.133) | copy-start | bytes 21508
  818.1 78.2 %copy-start.87 = (f32[2,56]{1,0:T(2,128)S(1)}, f32[2,56]{1,0:T(2,128)}, u32[]{:S(2)}) copy-start(f32[2,56]{1,0:T(2,128)} %param.47) | copy-start | bytes 1348
  818.2 78.2 %copy-start.88 = (f32[2,56]{1,0:T(2,128)S(1)}, f32[2,56]{1,0:T(2,128)}, u32[]{:S(2)}) copy-start(f32[2,56]{1,0:T(2,128)} %param.43) | copy-start | bytes 1348
  818.2 83.9 %copy-start.97 = (f32[7]{0:T(128)S(1)}, f32[7]{0:T(128)}, u32[]{:S(2)}) copy-start(f32[7]{0:T(128)} %stack.155) | copy-start | bytes 88
  818.2 132.7 %copy-start.2 = (f32[128,1792]{1,0:T(8,128)S(1)}, f32[128,1792]{1,0:T(8,128)}, u32[]{:S(2)}) copy-start(f32[128,1792]{1,0:T(8,128)} %copy-done.1) | copy-start | bytes 2752516
  818.2 132.7 %copy-start.53 = (f32[1792]{0:T(1024)S(1)}, f32[1792]{0:T(1024)}, u32[]{:S(2)}) copy-start(f32[1792]{0:T(1024)} %copy-done.52) | copy-start | bytes 21508
  818.2 132.7 %copy-start.75 = (f32[128]{0:T(128)S(1)}, f32[128]{0:T(128)}, u32[]{:S(2)}) copy-start(f32[128]{0:T(128)} %copy-done.73) | copy-start | bytes 1540
  818.2 132.7 %copy-start.91 = (f32[128]{0:T(128)S(1)}, f32[128]{0:T(128)}, u32[]{:S(2)}) copy-start(f32[128]{0:T(128)} %copy-done.90) | copy-start | bytes 1540
  941.2 12.8 %copy-start.57 = (f32[2,7]{1,0:T(2,128)}, f32[2,7]{1,0:T(2,128)S(1)}, u32[]{:S(2)}) copy-start(f32[2,7]{1,0:T(2,128)S(1)} %sqrt.31) | copy-start | bytes 172
  (72 other events, 233.5 us)
Sparse Core Ops, SparseCore 0:
  9.9 37.5 all-gather.18
  159.1 87.6 all-gather.20
  249.2 32.8 all-gather.12
  284.1 46.9 all-gather.14
  332.8 33.1 all-gather.22
  542.6 36.9 all-gather.16
where the time goes:
time: 977 us; the launch traced here: 969 us
  waiting for transfers between devices  358 us (37%)
  blocking collectives  264 us (27%)
  local copies, waits for them, and re-layouts  96.8 us (10%)
  other arithmetic  90.9 us (9%)
  matrix products  80.6 us (8%)
  starting transfers between devices  52.7 us (5%)
  between operations  25.6 us (3%)
    all_to_all x3, waiting for transfers between devices, scatter_sum(): lax.all_to_all(values.reshape(ctx, rows // ctx, columns), 'ctx', 0, 0)  107 us
    all_to_all x2, waiting for transfers between devices, return_columns(): swapped = lax.all_to_all(pieces, 'wsh', 1, 0)  92.5 us
    all_gather x4, waiting for transfers between devices, gather_rows(): return lax.all_gather(values, 'ctx', axis=0, tiled=True)  70.3 us
    all_gather x1, blocking collectives, body(): lax.all_gather(jnp.stack([premix, prefeed]).astype(bf16), BOTH, axis=1, t...  69.3 us
    unnamed x2, blocking collectives  57.4 us
    all_to_all x1, blocking collectives, scatter_sum(): lax.all_to_all(values.reshape(ctx, rows // ctx, columns), 'ctx', 0, 0)  47.2 us
    psum x1, blocking collectives, update(): totals = lax.psum(jnp.stack([weight_sums, step_sums]), BOTH)  39.1 us
    all_gather x1, waiting for transfers between devices, body(): shrink_own = lax.all_gather(shrink.astype(bf16), 'wsh', axis=0, tiled=True)  38.6 us
  transfers between devices with their start and end apart: 17, of which 12 were waited for; matrix products, arithmetic and copies ran while one was open for 17% of the time, Pallas kernels for 0%

commit v1 on v0

--- a/solution.py
+++ b/solution.py
@@ -18,6 +18,18 @@
 f32 = jnp.float32
 bf16 = jnp.bfloat16
 BOTH = ("ctx", "wsh")
+
+
+def collect(x, axis, dim):
+    ways, here, step = (lax.axis_size(axis), lax.axis_index(axis), x.shape[dim])
+    line, have = (x, 1)
+    while have < ways:
+        line = jnp.concatenate(
+            [line, lax.ppermute(line, axis, [(d, (d - have) % ways) for d in range(ways)])],
+            axis=dim,
+        )
+        have = 2 * have
+    return jnp.roll(line, here * step, axis=dim)
 
 
 def mm(left, right):
@@ -201,9 +213,7 @@
             )
 
         in_parts, ex_parts = ((QK, QK, width), (feed, feed))
-        gains = lax.all_gather(
-            jnp.stack([premix, prefeed]).astype(bf16), BOTH, axis=1, tiled=True
-        ).astype(f32)
+        gains = collect(jnp.stack([premix, prefeed]).astype(bf16), BOTH, 1).astype(f32)
         gain_one, gain_two = (gains[0], gains[1])
         taps = lax.all_gather(filters.astype(bf16), "wsh", axis=1, tiled=True).astype(f32)
         inward_own = gather_columns(inward.astype(bf16), in_parts, ctx)

time: 977 us -> 939 us (0.961)
  blocking collectives: 264 us -> 194 us
  waiting for transfers between devices: 358 us -> 373 us
  starting transfers between devices: 52.7 us -> 63.1 us
    all_gather x1 -> x0, blocking collectives: 69.3 us -> none  [body(): lax.all_gather(jnp.stack([premix, prefeed]).astype(bf16), BOTH, axis=1, t...]
    ppermute x0 -> x5, waiting for transfers between devices: none -> 16 us  [collect(): lax.ppermute(line, axis, [(d, (d - have) % ways) for d in range(ways)])]
    ppermute x0 -> x5, starting transfers between devices: none -> 10.3 us  [collect(): lax.ppermute(line, axis, [(d, (d - have) % ways) for d in range(ways)])]
  transfers between devices with their start and end apart: 17 -> 22, of which waited for: 12 -> 15; matrix products, arithmetic and copies ran while one was open for 17% -> 19% of each run, Pallas kernels for 0% -> 0%
where the time goes in v1:
time: 939 us; the launch traced here: 930 us
  waiting for transfers between devices  373 us (40%)
  blocking collectives  194 us (21%)
  local copies, waits for them, and re-layouts  99.9 us (11%)
  other arithmetic  93.8 us (10%)
  matrix products  80.6 us (9%)
  starting transfers between devices  63.1 us (7%)
  between operations  25.9 us (3%)
    all_to_all x3, waiting for transfers between devices, scatter_sum(): lax.all_to_all(values.reshape(ctx, rows // ctx, columns), 'ctx', 0, 0)  107 us
    all_to_all x2, waiting for transfers between devices, return_columns(): swapped = lax.all_to_all(pieces, 'wsh', 1, 0)  92.3 us
    all_gather x4, waiting for transfers between devices, gather_rows(): return lax.all_gather(values, 'ctx', axis=0, tiled=True)  70.3 us
    unnamed x2, blocking collectives  57.4 us
    all_to_all x1, blocking collectives, scatter_sum(): lax.all_to_all(values.reshape(ctx, rows // ctx, columns), 'ctx', 0, 0)  45.9 us
    psum x1, blocking collectives, update(): totals = lax.psum(jnp.stack([weight_sums, step_sums]), BOTH)  39.1 us
    all_gather x1, waiting for transfers between devices, body(): shrink_own = lax.all_gather(shrink.astype(bf16), 'wsh', axis=0, tiled=True)  38.6 us
    dot_general x4, matrix products, mm_nt(): lax.dot_general(left, right, (((1,), (1,)), ((), ())), preferred_element_...  26.4 us
  transfers between devices with their start and end apart: 22, of which 15 were waited for; matrix products, arithmetic and copies ran while one was open for 19% of the time, Pallas kernels for 0%

profile of v1, /device:TPU:0, one launch (start us, length us, event | category | flops | bytes accessed | tf_op | source)
XLA Modules:
  0.0 930.2 jit_solution(15100158912243776062)
XLA Ops:
  12.4 5.2 all-to-all-start
  18.8 6.0 collective-permute-start
  25.3 7.6 all-gather.4
  40.6 18.3 %all_gather.37 = bf16[224,1792]{1,0:T(8,128)(2,1)} all-gather(bf16[56,1792]{1,0:T(8,128)(2,1)S(1)} %get-tuple-element.311), channel_id=1, replica_groups=mesh['ctx'=8,'wsh'=4] {'wsh'}, dimensions={0}, use_global_device_ids=true | all-gather | bytes 1003520 | tf_op jit(solution)/shard_map/all_gather | solution.py:220
  65.6 4.3 all-to-all-start.2
  74.0 11.3 %collective-permute-done.3 = bf16[2,448]{1,0:T(2,128)(2,1)S(1)} collective-permute-done((bf16[2,448]{1,0:T(2,128)(2,1)S(1)}, bf16[2,448]{1,0:T(2,128)(2,1)S(1)}, u32[]{:S(2)}, u32[]{:S(2)}) %collective-permute-start.3) | collective-permute-done | bytes 1824 | tf_op jit(solution)/shard_map/ppermute | solution.py:28
  91.8 25.3 %all-gather.1 = bf16[8,224,288]{2,0,1:T(8,128)(2,1)S(1)} all-gather(bf16[8,56,288]{2,0,1:T(8,128)(2,1)S(1)} %copy.315), channel_id=3, replica_groups=mesh['ctx'=8,'wsh'=4] {'wsh'}, dimensions={1}, use_global_device_ids=true | all-gather | bytes 1290240 | tf_op jit(solution)/shard_map/all_gather | solution.py:94
  148.0 45.9 %all_to_all.68 = bf16[8,128,1792]{2,1,0:T(8,128)(2,1)S(1)} all-to-all(bf16[8,128,1792]{2,1,0:T(8,128)(2,1)S(1)} %bitcast.347), channel_id=1, replica_groups=mesh['ctx'=8,'wsh'=4] {'ctx'}, dimensions={0} | all-to-all | bytes 7340032 | tf_op jit(solution)/shard_map/all_to_all | solution.py:66
  198.9 8.9 all-gather.20.cloned.1.call-done
  207.8 35.3 %all-gather.12.cloned.1.call-done = bf16[1024,1792]{1,0:T(8,128)(2,1)} async-done(((bf16[128,1792]{1,0:T(8,128)(2,1)}), bf16[1024,1792]{1,0:T(8,128)(2,1)}) %all-gather.12.cloned.1.call-update) | async-done | bytes 3670032 | tf_op jit(solution)/shard_map/all_gather | solution.py:61
  243.1 10.4 %fusion.142 = f32[1024,1216]{0,1:T(8,128)} fusion(bf16[1024,1792]{1,0:T(8,128)(2,1)} %all-gather.12.cloned.1.call-done, bf16[1792,1216]{1,0:T(8,128)(2,1)} %bitcast.404), kind=kOutput, calls=%fused_computation.310 | convolution fusion | flops 4462739456 | bytes 13008896 | tf_op jit(solution)/shard_map/dot_general | solution.py:36
  253.5 38.6 %all-gather.14.cloned.1.call-done = bf16[608,1792]{1,0:T(8,128)(2,1)} async-done(((bf16[152,1792]{1,0:T(8,128)(2,1)}), bf16[608,1792]{1,0:T(8,128)(2,1)}) %all-gather.14.cloned.1.call-update) | async-done | bytes 2179088 | tf_op jit(solution)/shard_map/all_gather | solution.py:222
  292.1 34.9 %all-gather.22.cloned.1.call-done = bf16[1,1024,1792]{2,1,0:T(8,128)(2,1)} async-done(((bf16[1,128,1792]{2,1,0:T(8,128)(2,1)}), bf16[1,1024,1792]{2,1,0:T(8,128)(2,1)}) %all-gather.22.cloned.1.call-update) | async-done | bytes 3670032 | tf_op jit(solution)/shard_map/all_gather | solution.py:61
  327.1 8.4 multiply_convert_fusion.2
  335.4 9.7 %convolution_convert_fusion.2 = bf16[1024,1792]{1,0:T(8,128)(2,1)} fusion(bf16[1792,1216]{1,0:T(8,128)(2,1)} %bitcast.405, bf16[1024,608]{0,1:T(8,128)(2,1)S(1)} %get-tuple-element.274, bf16[1024,608]{0,1:T(8,128)(2,1)S(1)} %get-tuple-element.273), kind=kOutput, calls=%fused_computation.18 | convolution fusion | flops 4469555200 | bytes 10518528 | tf_op jit(solution)/shard_map/dot_general | solution.py:40
  345.1 4.7 all-to-all-start.4
  349.9 6.9 convolution_convert_fusion.3
  356.8 36.6 %all-to-all-done.4 = bf16[8,128,1792]{2,1,0:T(8,128)(2,1)} async-done(((bf16[8,128,1792]{2,1,0:T(8,128)(2,1)}), bf16[8,128,1792]{2,1,0:T(8,128)(2,1)}, u32[]{:S(2)}, u32[]{:S(2)}) %all-to-all-start.4) | async-done | bytes 3670048 | tf_op jit(solution)/shard_map/all_to_all | solution.py:66
  393.3 4.5 all-to-all-start.3
  397.8 6.2 fusion.7
  404.0 37.3 %all-to-all-done.3 = bf16[8,128,1792]{2,1,0:T(8,128)(2,1)} async-done(((bf16[8,128,1792]{2,1,0:T(8,128)(2,1)}), bf16[8,128,1792]{2,1,0:T(8,128)(2,1)}, u32[]{:S(2)}, u32[]{:S(2)}) %all-to-all-start.3) | async-done | bytes 3670048 | tf_op jit(solution)/shard_map/all_to_all | solution.py:66
  441.3 4.6 all-to-all-start.11
  445.9 9.6 %convolution_convert_fusion = bf16[1792,1216]{0,1:T(8,128)(2,1)} fusion(bf16[1024,1792]{1,0:T(8,128)(2,1)} %all-gather.12.cloned.1.call-done, bf16[1024,608]{0,1:T(8,128)(2,1)} %copy-done.106, bf16[1024,608]{0,1:T(8,128)(2,1)} %copy-done.105), kind=kOutput, calls=%fused_computation.7 | convolution fusion | flops 4469899264 | bytes 10518528 | tf_op jit(solution)/shard_map/dot_general | solution.py:44
  455.5 7.2 copy.365
  462.7 4.8 copy.366
  467.5 25.6 %all-to-all-done.11 = bf16[4,152,1792]{2,1,0:T(8,128)(2,1)} async-done(((bf16[4,152,1792]{2,1,0:T(8,128)(2,1)}), bf16[4,152,1792]{2,1,0:T(8,128)(2,1)}, u32[]{:S(2)}, u32[]{:S(2)}) %all-to-all-start.11) | async-done | bytes 2179104 | tf_op jit(solution)/shard_map/all_to_all | solution.py:110
  493.2 4.9 all-to-all-start.9
  506.6 5.1 stack.155
  519.2 80.1 %all-to-all-done.9 = bf16[1,8,4,56,1216]{4,3,1,0,2:T(8,128)(2,1)} async-done(((bf16[1,8,4,56,1216]{4,3,1,0,2:T(8,128)(2,1)}), bf16[1,8,4,56,1216]{4,3,1,0,2:T(8,128)(2,1)}, u32[]{:S(2)}, u32[]{:S(2)}) %all-to-all-start.9) | async-done | bytes 4358176 | tf_op jit(solution)/shard_map/all_to_all | solution.py:101
  599.3 4.4 reduce_sum.346
  603.6 4.9 all-to-all-start.10
  615.2 9.9 %all-to-all-done.10 = bf16[8,56,1216]{2,1,0:T(8,128)(2,1)} async-done(((bf16[8,56,1216]{2,1,0:T(8,128)(2,1)}), bf16[8,56,1216]{2,1,0:T(8,128)(2,1)}, u32[]{:S(2)}, u32[]{:S(2)}) %all-to-all-start.10) | async-done | bytes 1089568 | tf_op jit(solution)/shard_map/all_to_all | solution.py:103
  631.3 4.4 fusion.143
  638.6 4.4 multiply_reduce_fusion.6
  682.9 4.5 convolution_convert_fusion.5
  690.4 4.3 all-to-all-start.6
  694.7 4.5 fusion.11
  703.9 6.9 multiply_reduce_fusion
  712.7 12.2 %all-to-all-done.6 = bf16[1,8,4,56,288]{4,3,1,0,2:T(8,128)(2,1)} async-done(((bf16[1,8,4,56,288]{4,3,1,0,2:T(8,128)(2,1)}), bf16[1,8,4,56,288]{4,3,1,0,2:T(8,128)(2,1)}, u32[]{:S(2)}, u32[]{:S(2)}) %all-to-all-start.6) | async-done | bytes 1032224 | tf_op jit(solution)/shard_map/all_to_all | solution.py:101
  724.9 4.2 all-to-all-start.8
  729.2 4.0 pad_maximum_fusion
  733.2 15.3 %all-reduce.12 = f32[3,224]{1,0:T(4,128)} all-reduce(f32[3,224]{1,0:T(4,128)S(1)} %pad_maximum_fusion.13), channel_id=7, replica_groups=mesh['ctx'=8,'wsh'=4] {'wsh'}, use_global_device_ids=true, to_apply=%region_19.21.clone | all-reduce | flops 672 | bytes 5376
  750.9 5.2 all-to-all-start.7
  763.9 4.7 all-to-all-start.5
  779.2 32.9 %all-to-all-done.5 = bf16[8,128,1792]{2,1,0:T(8,128)(2,1)} async-done(((bf16[8,128,1792]{2,1,0:T(8,128)(2,1)}), bf16[8,128,1792]{2,1,0:T(8,128)(2,1)}, u32[]{:S(2)}, u32[]{:S(2)}) %all-to-all-start.5) | async-done | bytes 3670048 | tf_op jit(solution)/shard_map/all_to_all | solution.py:66
  815.1 42.1 %all-reduce.11 = f32[2,1792]{1,0:T(2,128)S(1)} all-reduce(f32[2,1792]{1,0:T(2,128)S(1)} %pad_maximum_fusion.12), channel_id=6, replica_groups=mesh['ctx'=8,'wsh'=4] {'ctx','wsh'}, use_global_device_ids=true, to_apply=%region_14.16.clone | all-reduce | flops 3584 | bytes 28672
  858.4 4.6 stack.164
  863.0 39.1 %psum.7 = f32[2,7]{1,0:T(2,128)S(1)} all-reduce(f32[2,7]{1,0:T(2,128)S(1)} %pad_maximum_fusion.19), channel_id=1, replica_groups=mesh['ctx'=8,'wsh'=4] {'ctx','wsh'}, use_global_device_ids=true, to_apply=%region_37.39 | all-reduce | flops 14 | bytes 112 | tf_op jit(solution)/shard_map/psum | solution.py:360
  (426 shorter events, 183.9 us)
Async XLA Ops:
  7.2 115.4 %all-gather.18.cloned.1.call-start = ((), (), s32[]{:S(2)}) async-start(), calls=%async_computation.15 | async-start | bytes 4128768 | tf_op jit(solution)/shard_map/all_gather | solution.py:61
  7.9 16.8 %copy-start.70 = (f32[3,56]{1,0:T(4,128)S(1)}, f32[3,56]{1,0:T(4,128)}, u32[]{:S(2)}) copy-start(f32[3,56]{1,0:T(4,128)} %param.38) | copy-start | bytes 2020
  8.0 25.0 %copy-start.8 = (f32[56,9728]{1,0:T(8,128)S(1)}, f32[56,9728]{1,0:T(8,128)}, u32[]{:S(2)}) copy-start(f32[56,9728]{1,0:T(8,128)} %param.41) | copy-start | bytes 6537220
  12.4 53.1 %all-to-all-start = ((bf16[8,56,288]{2,1,0:T(8,128)(2,1)}), bf16[8,56,288]{2,1,0:T(8,128)(2,1)}, u32[]{:S(2)}, u32[]{:S(2)}) async-start(bf16[8,56,288]{2,1,0:T(8,128)(2,1)} %maximum_bitcast_fusion.1), calls=%async_computation | async-start | bytes 688128 | tf_op jit(solution)/shard_map/all_to_all | solution.py:93
  18.2 16.1 %copy-start.73 = (bf16[1,56]{1,0:T(2,128)(2,1)}, bf16[1,56]{1,0:T(2,128)(2,1)S(1)}, u32[]{:S(2)}) copy-start(bf16[1,56]{1,0:T(2,128)(2,1)S(1)} %get-tuple-element.355) | copy-start | bytes 340
  18.2 16.1 %copy-start.75 = (bf16[1,56]{1,0:T(2,128)(2,1)}, bf16[1,56]{1,0:T(2,128)(2,1)S(1)}, u32[]{:S(2)}) copy-start(bf16[1,56]{1,0:T(2,128)(2,1)S(1)} %get-tuple-element.359) | copy-start | bytes 340
  18.8 40.8 %collective-permute-start = (bf16[2,56]{1,0:T(2,128)(2,1)}, bf16[2,56]{1,0:T(2,128)(2,1)}, u32[]{:S(2)}, u32[]{:S(2)}) collective-permute-start(bf16[2,56]{1,0:T(2,128)(2,1)} %pad_maximum_fusion.20), channel_id=1, source_target_pairs={{0,31},{1,0},{2,1},{3,2},{4,3},{5,4},{6,5},{7,6},{8,7},{9,8},{10,9... | collective-permute-start | bytes 680 | tf_op jit(solution)/shard_map/ppermute | solution.py:28
  38.6 20.3 %copy-start.102 = (s32[16]{0:T(128)S(1)}, s32[16]{0:T(128)}, u32[]{:S(2)}) copy-start(s32[16]{0:T(128)} %param.35) | copy-start | bytes 196
  38.6 21.0 %copy-start.74 = (bf16[1,56]{1,0:T(2,128)(2,1)S(1)}, bf16[1,56]{1,0:T(2,128)(2,1)}, u32[]{:S(2)}) copy-start(bf16[1,56]{1,0:T(2,128)(2,1)} %copy-done.73) | copy-start | bytes 340
  38.6 21.0 %copy-start.76 = (bf16[1,56]{1,0:T(2,128)(2,1)S(1)}, bf16[1,56]{1,0:T(2,128)(2,1)}, u32[]{:S(2)}) copy-start(bf16[1,56]{1,0:T(2,128)(2,1)} %copy-done.75) | copy-start | bytes 340
  39.1 92.0 %copy-start.11 = (f32[8,128,384]{2,1,0:T(8,128)}, f32[8,128,384]{2,1,0:T(8,128)S(1)}, u32[]{:S(2)}) copy-start(f32[8,128,384]{2,1,0:T(8,128)S(1)} %and_convert_fusion) | copy-start | bytes 4718596
  60.3 4.5 collective-permute-start.1
  60.9 29.9 %copy-start.80 = (pred[16]{0:T(512)(128)(4,1)}, pred[16]{0:T(512)(128)(4,1)S(1)}, u32[]{:S(2)}) copy-start(pred[16]{0:T(512)(128)(4,1)S(1)} %get-tuple-element.362) | copy-start | bytes 52
  65.5 4.3 collective-permute-start.2
  65.6 56.5 %all-to-all-start.2 = ((bf16[8,56,1216]{2,1,0:T(8,128)(2,1)}), bf16[8,56,1216]{2,1,0:T(8,128)(2,1)}, u32[]{:S(2)}, u32[]{:S(2)}) async-start(bf16[8,56,1216]{2,1,0:T(8,128)(2,1)} %maximum_bitcast_fusion), calls=%async_computation.2 | async-start | bytes 2293760 | tf_op jit(solution)/shard_map/all_to_all | solution.py:93
  69.8 137.9 %all-gather.20.cloned.1.call-start = ((), (), s32[]{:S(2)}) async-start(), calls=%async_computation.16 | async-start | bytes 5734400 | tf_op jit(solution)/shard_map/all_gather | solution.py:94
  70.6 14.6 %collective-permute-start.3 = (bf16[2,448]{1,0:T(2,128)(2,1)S(1)}, bf16[2,448]{1,0:T(2,128)(2,1)S(1)}, u32[]{:S(2)}, u32[]{:S(2)}) collective-permute-start(bf16[2,448]{1,0:T(2,128)(2,1)S(1)} %pad_maximum_fusion.15), channel_id=1, source_target_pairs={{0,24},{1,25},{2,26},{3,27},{4,28},{5,29},{6,30},{7,31},{8,0},{9,1... | collective-permute-start | bytes 5384 | tf_op jit(solution)/shard_map/ppermute | solution.py:28
  86.1 3.7 collective-permute-start.4
  90.7 410.9 %copy-start.52 = (f32[1792]{0:T(1024)}, f32[1792]{0:T(1024)S(1)}, u32[]{:S(2)}) copy-start(f32[1792]{0:T(1024)S(1)} %get-tuple-element.250) | copy-start | bytes 21508
  90.8 591.2 %copy-start.55 = (f32[1792]{0:T(1024)}, f32[1792]{0:T(1024)S(1)}, u32[]{:S(2)}) copy-start(f32[1792]{0:T(1024)S(1)} %get-tuple-element.249) | copy-start | bytes 21508
  122.1 121.0 %all-gather.12.cloned.1.call-start = ((), (), s32[]{:S(2)}) async-start(), calls=%async_computation.12 | async-start | bytes 4128768 | tf_op jit(solution)/shard_map/all_gather | solution.py:61
  130.5 12.2 %copy-start.4 = (bf16[16,64,288]{2,1,0:T(8,128)(2,1)}, bf16[16,64,288]{2,1,0:T(8,128)(2,1)S(1)}, u32[]{:S(2)}) copy-start(bf16[16,64,288]{2,1,0:T(8,128)(2,1)S(1)} %broadcast_select_fusion.1) | copy-start | bytes 1769476
  196.6 95.5 %all-gather.14.cloned.1.call-start = ((), (), s32[]{:S(2)}) async-start(), calls=%async_computation.13 | async-start | bytes 2723840 | tf_op jit(solution)/shard_map/all_gather | solution.py:222
  198.3 128.8 %all-gather.22.cloned.1.call-start = ((), (), s32[]{:S(2)}) async-start(), calls=%async_computation.17 | async-start | bytes 4128768 | tf_op jit(solution)/shard_map/all_gather | solution.py:61
  345.1 48.2 %all-to-all-start.4 = ((bf16[8,128,1792]{2,1,0:T(8,128)(2,1)}), bf16[8,128,1792]{2,1,0:T(8,128)(2,1)}, u32[]{:S(2)}, u32[]{:S(2)}) async-start(bf16[8,128,1792]{2,1,0:T(8,128)(2,1)} %bitcast.359), calls=%async_computation.4 | async-start | bytes 7340032 | tf_op jit(solution)/shard_map/all_to_all | solution.py:66
  393.3 48.0 %all-to-all-start.3 = ((bf16[8,128,1792]{2,1,0:T(8,128)(2,1)}), bf16[8,128,1792]{2,1,0:T(8,128)(2,1)}, u32[]{:S(2)}, u32[]{:S(2)}) async-start(bf16[8,128,1792]{2,1,0:T(8,128)(2,1)} %bitcast.358), calls=%async_computation.3 | async-start | bytes 7340032 | tf_op jit(solution)/shard_map/all_to_all | solution.py:66
  441.3 51.8 %all-to-all-start.11 = ((bf16[4,152,1792]{2,1,0:T(8,128)(2,1)}), bf16[4,152,1792]{2,1,0:T(8,128)(2,1)}, u32[]{:S(2)}, u32[]{:S(2)}) async-start(bf16[4,152,1792]{2,1,0:T(8,128)(2,1)} %bitcast.361), calls=%async_computation.11 | async-start | bytes 4358144 | tf_op jit(solution)/shard_map/all_to_all | solution.py:110
  493.2 106.1 %all-to-all-start.9 = ((bf16[1,8,4,56,1216]{4,3,1,0,2:T(8,128)(2,1)}), bf16[1,8,4,56,1216]{4,3,1,0,2:T(8,128)(2,1)}, u32[]{:S(2)}, u32[]{:S(2)}) async-start(bf16[1,8,4,56,1216]{4,3,1,0,2:T(8,128)(2,1)} %copy.366), calls=%async_computation.9 | async-start | bytes 9175040 | tf_op jit(solution)/shard_map/all_to_all | solution.py:101
  498.1 133.2 %all-gather.16.cloned.1.call-start = ((), (), s32[]{:S(2)}) async-start(), calls=%async_computation.14 | async-start | bytes 4128768 | tf_op jit(solution)/shard_map/all_gather | solution.py:61
  519.2 92.9 %copy-start.5 = (f32[152,1792]{1,0:T(8,128)}, f32[152,1792]{1,0:T(8,128)S(1)}, u32[]{:S(2)}) copy-start(f32[152,1792]{1,0:T(8,128)S(1)} %convert_reduce_fusion.4) | copy-start | bytes 3268612
  603.6 21.5 %all-to-all-start.10 = ((bf16[8,56,1216]{2,1,0:T(8,128)(2,1)}), bf16[8,56,1216]{2,1,0:T(8,128)(2,1)}, u32[]{:S(2)}, u32[]{:S(2)}) async-start(bf16[8,56,1216]{2,1,0:T(8,128)(2,1)} %reduce_sum.346), calls=%async_computation.10 | async-start | bytes 2293760 | tf_op jit(solution)/shard_map/all_to_all | solution.py:103
  690.4 34.5 %all-to-all-start.6 = ((bf16[1,8,4,56,288]{4,3,1,0,2:T(8,128)(2,1)}), bf16[1,8,4,56,288]{4,3,1,0,2:T(8,128)(2,1)}, u32[]{:S(2)}, u32[]{:S(2)}) async-start(bf16[1,8,4,56,288]{4,3,1,0,2:T(8,128)(2,1)} %copy.358), calls=%async_computation.6 | async-start | bytes 2752512 | tf_op jit(solution)/shard_map/all_to_all | solution.py:101
  724.9 26.0 %all-to-all-start.8 = ((bf16[4,56,1792]{2,1,0:T(8,128)(2,1)}), bf16[4,56,1792]{2,1,0:T(8,128)(2,1)}, u32[]{:S(2)}, u32[]{:S(2)}) async-start(bf16[4,56,1792]{2,1,0:T(8,128)(2,1)} %bitcast.368), calls=%async_computation.8 | async-start | bytes 1605632 | tf_op jit(solution)/shard_map/all_to_all | solution.py:110
  733.2 23.0 %copy-start.39 = (bf16[1792,288]{0,1:T(8,128)(2,1)S(1)}, bf16[1792,288]{0,1:T(8,128)(2,1)}, u32[]{:S(2)}) copy-start(bf16[1792,288]{0,1:T(8,128)(2,1)} %copy-done.38) | copy-start | bytes 3096580
  733.2 23.0 %copy-start.41 = (bf16[16,64,288]{2,1,0:T(8,128)(2,1)S(1)}, bf16[16,64,288]{2,1,0:T(8,128)(2,1)}, u32[]{:S(2)}) copy-start(bf16[16,64,288]{2,1,0:T(8,128)(2,1)} %copy-done.40) | copy-start | bytes 1769476
  750.9 13.0 %all-to-all-start.7 = ((bf16[8,56,288]{2,1,0:T(8,128)(2,1)}), bf16[8,56,288]{2,1,0:T(8,128)(2,1)S(1)}, u32[]{:S(2)}, u32[]{:S(2)}) async-start(bf16[8,56,288]{2,1,0:T(8,128)(2,1)} %reduce_sum.341), calls=%async_computation.7 | async-start | bytes 688128 | tf_op jit(solution)/shard_map/all_to_all | solution.py:103
  763.9 48.1 %all-to-all-start.5 = ((bf16[8,128,1792]{2,1,0:T(8,128)(2,1)}), bf16[8,128,1792]{2,1,0:T(8,128)(2,1)}, u32[]{:S(2)}, u32[]{:S(2)}) async-start(bf16[8,128,1792]{2,1,0:T(8,128)(2,1)} %bitcast.357), calls=%async_computation.5 | async-start | bytes 7340032 | tf_op jit(solution)/shard_map/all_to_all | solution.py:66
  779.1 35.6 %copy-start.56 = (f32[1792]{0:T(1024)S(1)}, f32[1792]{0:T(1024)}, u32[]{:S(2)}) copy-start(f32[1792]{0:T(1024)} %copy-done.55) | copy-start | bytes 21508
  779.1 35.6 %copy-start.96 = (f32[128]{0:T(128)S(1)}, f32[128]{0:T(128)}, u32[]{:S(2)}) copy-start(f32[128]{0:T(128)} %add_rsqrt_fusion.1) | copy-start | bytes 1540
  779.1 35.9 %copy-start.60 = (f32[1,1792]{1,0:T(1,128)S(1)}, f32[1,1792]{1,0:T(1,128)}, u32[]{:S(2)}) copy-start(f32[1,1792]{1,0:T(1,128)} %stack.133) | copy-start | bytes 21508
  779.1 78.2 %copy-start.91 = (f32[2,56]{1,0:T(2,128)S(1)}, f32[2,56]{1,0:T(2,128)}, u32[]{:S(2)}) copy-start(f32[2,56]{1,0:T(2,128)} %param.47) | copy-start | bytes 1348
  779.1 78.2 %copy-start.92 = (f32[2,56]{1,0:T(2,128)S(1)}, f32[2,56]{1,0:T(2,128)}, u32[]{:S(2)}) copy-start(f32[2,56]{1,0:T(2,128)} %param.43) | copy-start | bytes 1348
  779.1 83.9 %copy-start.101 = (f32[7]{0:T(128)S(1)}, f32[7]{0:T(128)}, u32[]{:S(2)}) copy-start(f32[7]{0:T(128)} %stack.155) | copy-start | bytes 88
  779.1 132.9 %copy-start.2 = (f32[128,1792]{1,0:T(8,128)S(1)}, f32[128,1792]{1,0:T(8,128)}, u32[]{:S(2)}) copy-start(f32[128,1792]{1,0:T(8,128)} %copy-done.1) | copy-start | bytes 2752516
  779.1 132.9 %copy-start.53 = (f32[1792]{0:T(1024)S(1)}, f32[1792]{0:T(1024)}, u32[]{:S(2)}) copy-start(f32[1792]{0:T(1024)} %copy-done.52) | copy-start | bytes 21508
  779.1 132.9 %copy-start.79 = (f32[128]{0:T(128)S(1)}, f32[128]{0:T(128)}, u32[]{:S(2)}) copy-start(f32[128]{0:T(128)} %copy-done.77) | copy-start | bytes 1540
  779.1 132.9 %copy-start.95 = (f32[128]{0:T(128)S(1)}, f32[128]{0:T(128)}, u32[]{:S(2)}) copy-start(f32[128]{0:T(128)} %copy-done.94) | copy-start | bytes 1540
  902.1 13.1 %copy-start.57 = (f32[2,7]{1,0:T(2,128)}, f32[2,7]{1,0:T(2,128)S(1)}, u32[]{:S(2)}) copy-start(f32[2,7]{1,0:T(2,128)S(1)} %sqrt.31) | copy-start | bytes 172
  (81 other events, 324.6 us)
Sparse Core Ops, SparseCore 0:
  9.9 39.1 all-gather.17
  122.2 85.5 all-gather.19
  210.2 32.8 all-gather.11
  245.1 46.9 all-gather.13
  293.9 33.1 all-gather.21
  503.8 36.9 all-gather.15
